TPU v7x, 256 devices: a whole 4x4x8 slice. The times are simulated.
256 devices in a mesh: dp: 4 (over x), expert: 32 (over y, z), tensor: 2 (over core).
Axes of the slice: x: 4, y: 4, z: 8, core: 2. Of those that a mesh axis runs over, the one named last changes fastest.
Arguments:
- tokens: bfloat16 [16384, 2560], P(('dp', 'expert')), may hold values from -6 to 6
- norm_gain: float32 [2560], replicated, may hold values from 0.5 to 1.5
- expert_ids: int32 [16384, 6], P(('dp', 'expert')), may hold values from 0 to 31, all different within a row; in each aligned block of 128 rows (0 to 127, 128 to 255, ...) at most 48 rows name the same one
- route_weights: int32 [16384, 6], P(('dp', 'expert')), may hold values from 1 to 64
- w_gate: bfloat16 [32, 2560, 768], P('expert', None, 'tensor'), may hold values from -0.125 to 0.125
- w_up: bfloat16 [32, 2560, 768], P('expert', None, 'tensor'), may hold values from -0.125 to 0.125
- w_down: bfloat16 [32, 768, 2560], P('expert', 'tensor'), may hold values from -0.21875 to 0.21875
- shared_gate: bfloat16 [2560, 2048], P(None, ('dp', 'tensor')), may hold values from -0.125 to 0.125
- shared_up: bfloat16 [2560, 2048], P(None, ('dp', 'tensor')), may hold values from -0.125 to 0.125
- shared_down: bfloat16 [2048, 2560], P(('dp', 'tensor')), may hold values from -0.125 to 0.125
Outputs:
- mixed: bfloat16 [16384, 2560], P(('dp', 'expert'), 'tensor')
Inputs may be any that keep to these rules, and one draw needn't show every extreme that they name: `expert_ids`: each row names 6 different experts. In each aligned block of 128 rows (the rows of one index of dp+expert) no expert is named by more than 48 rows, a bound that some blocks reach.
All inputs are finite; a program needn't handle non-finite values.
Results may differ from a plain program's by a relative error of at most 0.011.
Values may be sent and summed in bfloat16 or wider, within the bound.
No kernel may reach another device: no remote copies, remote signals or barrier semaphores. Data moves between devices by JAX's collectives and lax.ppermute only.
A program may use at most 128 MiB of HBM per device.

v0:
```python
import jax
import jax.numpy as jnp
from jax import lax
from jax.sharding import PartitionSpec as P

D = 2560
EXPERTS = 32
TOP = 6
CAP = 48
EPSILON = 1e-06


def normalize(tokens, norm_gain):
    values = tokens.astype(jnp.float32)
    inverse = lax.rsqrt(jnp.mean(values * values, axis=1, keepdims=True) + EPSILON)
    return (values * inverse * norm_gain[None, :]).astype(jnp.bfloat16)


def slot_positions(expert_ids):
    flat_ids = expert_ids.reshape(-1)
    onehot = (flat_ids[:, None] == jnp.arange(EXPERTS, dtype=jnp.int32)[None, :]).astype(jnp.int32)
    earlier = jnp.cumsum(onehot, axis=0) - onehot
    return flat_ids * CAP + jnp.sum(earlier * onehot, axis=1)


def on_device(
    tokens,
    norm_gain,
    expert_ids,
    route_weights,
    w_gate,
    w_up,
    w_down,
    shared_gate,
    shared_up,
    shared_down,
):
    normed = normalize(tokens, norm_gain)
    tok_rows = normed.shape[0]
    tensor_count = lax.axis_size("tensor")
    half_width = D // tensor_count
    tensor_rank = lax.axis_index("tensor")
    owners = lax.axis_size("expert")
    exp_local = w_gate.shape[0]
    position = slot_positions(expert_ids)
    pair_count = position.shape[0]
    pair_token = jnp.arange(pair_count, dtype=jnp.int32) // TOP
    filler = jnp.full((EXPERTS * CAP,), -1, jnp.int32).at[position].set(pair_token)
    filled = filler >= 0
    safe_rows = jnp.maximum(filler, 0)
    source_rows = lax.dynamic_slice_in_dim(normed, tensor_rank * half_width, half_width, 1)
    outgoing = jnp.where(filled[:, None], source_rows[safe_rows], jnp.zeros((), jnp.bfloat16))
    outgoing = outgoing.reshape(EXPERTS, CAP, source_rows.shape[1])
    arrived = lax.all_to_all(outgoing, "expert", split_axis=0, concat_axis=0, tiled=True)
    arrived = lax.all_gather(arrived, "tensor", axis=2, tiled=True)
    slot_count = arrived.shape[1]
    grouped = arrived.reshape(owners, exp_local, slot_count, D)
    gate_value = jnp.einsum("jecd,edf->jecf", grouped, w_gate, preferred_element_type=jnp.float32)
    up_value = jnp.einsum("jecd,edf->jecf", grouped, w_up, preferred_element_type=jnp.float32)
    hidden = (jax.nn.silu(gate_value) * up_value).astype(jnp.bfloat16)
    partial_out = jnp.einsum("jecf,efd->jecd", hidden, w_down, preferred_element_type=jnp.float32)
    summed = lax.psum_scatter(
        partial_out.astype(jnp.bfloat16), "tensor", scatter_dimension=3, tiled=True
    )
    summed = summed.reshape(owners * exp_local, slot_count, half_width)
    result_rows = lax.all_to_all(summed, "expert", split_axis=0, concat_axis=0, tiled=True)
    piece_rows = lax.all_gather(normed, "dp", axis=0, tiled=True)
    gate_value = jnp.dot(piece_rows, shared_gate, preferred_element_type=jnp.float32)
    up_value = jnp.dot(piece_rows, shared_up, preferred_element_type=jnp.float32)
    shared_hidden = (jax.nn.silu(gate_value) * up_value).astype(jnp.bfloat16)
    start_row = jnp.int32(0)
    pieces = []
    for offset in range(tok_rows * lax.axis_size(("dp", "tensor")) // tok_rows):
        block_index = start_row // tok_rows + offset
        group_index = block_index // tensor_count
        column_index = block_index % tensor_count
        hidden_block = lax.dynamic_slice_in_dim(shared_hidden, group_index * tok_rows, tok_rows, 0)
        down_block = lax.dynamic_slice_in_dim(shared_down, column_index * half_width, half_width, 1)
        pieces.append(jnp.dot(hidden_block, down_block, preferred_element_type=jnp.float32))
    shared_part = lax.psum_scatter(
        jnp.concatenate(pieces, axis=0).astype(jnp.bfloat16),
        ("dp", "tensor"),
        scatter_dimension=0,
        tiled=True,
    ).astype(jnp.float32)
    table = result_rows.reshape(EXPERTS * CAP, half_width)
    picked = table[position].reshape(tok_rows, TOP, half_width).astype(jnp.float32)
    scales = route_weights.astype(jnp.float32) / 64.0
    routed = jnp.sum(scales[:, :, None] * picked, axis=1)
    return (shared_part + routed).astype(jnp.bfloat16)


def solution(mesh):
    placed = (
        P(("dp", "expert"), None),
        P(),
        P(("dp", "expert"), None),
        P(("dp", "expert"), None),
        P("expert", None, "tensor"),
        P("expert", None, "tensor"),
        P("expert", "tensor", None),
        P(None, ("dp", "tensor")),
        P(None, ("dp", "tensor")),
        P(("dp", "tensor"), None),
    )
    return jax.shard_map(
        on_device,
        mesh=mesh,
        in_specs=placed,
        out_specs=P(("dp", "expert"), "tensor"),
        check_vma=False,
    )
```

profile of v0, /device:TPU:2, one launch (start us, length us, event | category | flops | bytes accessed | tf_op | source)
XLA Modules:
  0.0 321.8 jit_solution(4597402215661047442)
XLA Ops:
  7.4 0.9 copy.14
  8.6 0.7 broadcast_multiply_fusion
  9.3 1.7 reduce-window.6
  11.0 0.3 slice_reduce_fusion
  11.7 3.4 %scatter_custom_fusion = s32[1536]{0:T(1024)S(1)} fusion(s32[768]{0:T(1024)S(1)} %fusion.53, s32[768]{0:T(1024)S(1)} %add_select_fusion, s32[]{:T(128)} %constant.415.clone.1), kind=kCustom, calls=%fused_computation.79 | custom fusion | bytes 6148 | tf_op jit(solution)/shard_map/scatter | solution.py:48
  15.2 1.3 fusion.22
  16.6 1.3 fusion.24
  17.9 6.0 %gather_fusion = bf16[1536,1280]{1,0:T(8,128)(2,1)} fusion(bf16[128,1280]{1,0:T(8,128)(2,1)S(1)} %constant_dynamic-slice_fusion, s32[2048]{0:T(1024)S(1)} %pad_clamp_fusion), kind=kCustom, calls=%fused_computation | custom fusion | bytes 7870464 | tf_op jit(solution)/shard_map/gather | solution.py:52
  24.0 2.4 broadcast_select_fusion
  26.3 101.1 %all_to_all.10 = bf16[32,48,1280]{2,1,0:T(8,128)(2,1)} all-to-all(bf16[32,48,1280]{2,1,0:T(8,128)(2,1)S(1)} %broadcast_select_fusion), channel_id=1, replica_groups=mesh['dp'=4,'expert'=32,'tensor'=2] {'expert'}, dimensions={0} | all-to-all | bytes 7864320 | tf_op jit(solution)/shard_map/all_to_all | solution.py:54
  127.5 21.8 %all-gather.5.cloned.1.call-done = bf16[32,48,2560]{2,1,0:T(8,128)(2,1)} async-done(((bf16[32,48,1280]{2,1,0:T(8,128)(2,1)}), bf16[32,48,2560]{2,1,0:T(8,128)(2,1)}) %all-gather.5.cloned.1.call-update) | async-done | bytes 7864336 | tf_op jit(solution)/shard_map/all_gather | solution.py:55
  149.3 9.4 %fusion.13 = f32[32,48,384]{2,1,0:T(8,128)} fusion(bf16[32,48,2560]{2,1,0:T(8,128)(2,1)} %all-gather.5.cloned.1.call-done, bf16[1,2560,384]{2,1,0:T(8,128)(2,1)} %param.15), kind=kOutput, calls=%fused_computation.30 | convolution fusion | flops 3019898880 | bytes 12189696 | tf_op jit(solution)/shard_map/jecd,edf->jecf/dot_general | solution.py:59
  158.7 13.5 %convert_bitcast_fusion = bf16[32,1,48,2560]{3,2,0,1:T(8,128)(2,1)} fusion(bf16[1,384,2560]{2,1,0:T(8,128)(2,1)S(1)} %copy-done, f32[32,48,384]{2,1,0:T(8,128)} %fusion.13, bf16[32,48,2560]{2,1,0:T(8,128)(2,1)} %all-gather.5.cloned.1.call-done, bf16[1,2560,384]{2,1,0:T(8,128)(2,1)} %param.14), kind=kOutput, calls=%fused_computation.3 | convolution fusion | flops 6047268864 | bytes 22020096 | tf_op jit(solution)/shard_map/jecf,efd->jecd/dot_general | solution.py:61
  172.3 0.5 all-gather.3.cloned.1.call-update
  172.9 21.6 %reduce-scatter.5.cloned.1.call-done = bf16[32,1,48,1280]{3,2,0,1:T(8,128)(2,1)} async-done(((bf16[32,1,48,2560]{3,2,0,1:T(8,128)(2,1)}), bf16[32,1,48,1280]{3,2,0,1:T(8,128)(2,1)}) %reduce-scatter.5.cloned.1.call-update) | async-done | bytes 3932176 | tf_op jit(solution)/shard_map/reduce_scatter | solution.py:62
  194.4 10.0 %all-to-all-start.1 = ((bf16[32,48,1280]{2,1,0:T(8,128)(2,1)}), bf16[32,48,1280]{2,1,0:T(8,128)(2,1)}, u32[]{:S(2)}, u32[]{:S(2)}) async-start(bf16[32,48,1280]{2,1,0:T(8,128)(2,1)} %bitcast.91), calls=%async_computation.3 | async-start | bytes 7864320 | tf_op jit(solution)/shard_map/all_to_all | solution.py:66
  204.7 7.9 %all-gather.3.cloned.1.call-done = bf16[512,2560]{1,0:T(8,128)(2,1)} async-done(((bf16[128,2560]{1,0:T(8,128)(2,1)}), bf16[512,2560]{1,0:T(8,128)(2,1)}) %all-gather.3.cloned.1.call-update) | async-done | bytes 2621456 | tf_op jit(solution)/shard_map/all_gather | solution.py:67
  212.6 3.1 fusion.55
  215.7 2.3 fusion.25
  218.0 1.0 fusion.7
  218.9 1.0 fusion.6
  219.9 1.0 fusion.5
  220.9 1.0 fusion.4
  221.9 1.0 fusion.3
  222.9 1.0 fusion.2
  223.9 1.0 fusion.1
  224.9 1.0 fusion
  226.0 70.2 %all-to-all-done.1 = bf16[32,48,1280]{2,1,0:T(8,128)(2,1)} async-done(((bf16[32,48,1280]{2,1,0:T(8,128)(2,1)}), bf16[32,48,1280]{2,1,0:T(8,128)(2,1)}, u32[]{:S(2)}, u32[]{:S(2)}) %all-to-all-start.1) | async-done | bytes 3932192 | tf_op jit(solution)/shard_map/all_to_all | solution.py:66
  296.2 7.8 %gather_fusion.1 = bf16[768,1280]{1,0:T(8,128)(2,1)} fusion(bf16[1536,1280]{1,0:T(8,128)(2,1)} %bitcast.21, s32[1024]{0:T(1024)S(1)} %pad_clamp_fusion.1), kind=kCustom, calls=%fused_computation.1 | custom fusion | bytes 3935232 | tf_op jit(solution)/shard_map/gather | solution.py:87
  304.0 4.5 %reshape.101 = f32[128,6,1280]{2,1,0:T(8,128)} reshape(bf16[768,1280]{1,0:T(8,128)(2,1)} %gather_fusion.1) | data formatting | bytes 5898240 | tf_op jit(solution)/shard_map/convert_element_type | solution.py:87
  308.5 4.1 %multiply_reduce_fusion = f32[128,1280]{1,0:T(8,128)S(1)} fusion(f32[128,6,1280]{2,1,0:T(8,128)} %reshape.101, f32[128,6]{1,0:T(8,128)S(1)} %copy.12), kind=kLoop, calls=%fused_computation.4 | loop fusion | flops 1802240 | bytes 4590592 | tf_op jit(solution)/shard_map/reduce_sum | solution.py:89
  312.7 1.8 add_convert_fusion
  (36 shorter events, 1.4 us)
Async XLA Ops:
  7.4 151.4 %copy-start = (bf16[1,384,2560]{2,1,0:T(8,128)(2,1)S(1)}, bf16[1,384,2560]{2,1,0:T(8,128)(2,1)}, u32[]{:S(2)}) copy-start(bf16[1,384,2560]{2,1,0:T(8,128)(2,1)} %param.16) | copy-start | bytes 5898244
  7.4 141.9 %all-gather.5.cloned.1.call-start = ((), (), s32[]{:S(2)}) async-start(), calls=%async_computation.6 | async-start | bytes 11796480 | tf_op jit(solution)/shard_map/all_gather | solution.py:55
  17.9 6.1 %copy-start.1 = (bf16[128,2560]{1,0:T(8,128)(2,1)}, bf16[128,2560]{1,0:T(8,128)(2,1)S(1)}, u32[]{:S(2)}) copy-start(bf16[128,2560]{1,0:T(8,128)(2,1)S(1)} %fusion.24) | copy-start | bytes 1966084
  127.5 67.0 %reduce-scatter.5.cloned.1.call-start = ((), (), s32[]{:S(2)}) async-start(), calls=%async_computation.7 | async-start | bytes 11796480 | tf_op jit(solution)/shard_map/reduce_scatter | solution.py:62
  172.3 40.3 %all-gather.3.cloned.1.call-start = ((), (), s32[]{:S(2)}) async-start(), calls=%async_computation.4 | async-start | bytes 3276800 | tf_op jit(solution)/shard_map/all_gather | solution.py:67
  194.4 101.8 %all-to-all-start.1 = ((bf16[32,48,1280]{2,1,0:T(8,128)(2,1)}), bf16[32,48,1280]{2,1,0:T(8,128)(2,1)}, u32[]{:S(2)}, u32[]{:S(2)}) async-start(bf16[32,48,1280]{2,1,0:T(8,128)(2,1)} %bitcast.91), calls=%async_computation.3 | async-start | bytes 7864320 | tf_op jit(solution)/shard_map/all_to_all | solution.py:66
  204.4 108.2 %reduce-scatter.3.cloned.1.call-start = ((), (), s32[]{:S(2)}) async-start(), calls=%async_computation.5 | async-start | bytes 2949120 | tf_op jit(solution)/shard_map/reduce_scatter | solution.py:80
  212.6 3.1 copy-start.3
  215.7 2.3 copy-start.4
  223.9 2.0 copy-start.2
Sparse Core Ops, SparseCore 0:
  127.6 21.6 all-gather.4
  172.4 21.9 reduce-scatter.4
Sparse Core Ops, SparseCore 1:
  174.6 37.9 all-gather.2
  225.9 35.7 reduce-scatter.2
where the time goes:
time: 322 us
  waiting for transfers between devices  122 us (38%)
  blocking collectives  101 us (31%)
  matrix products  36.2 us (11%)
  local copies, waits for them, and re-layouts  23.7 us (7%)
  between operations  15.1 us (5%)
  other arithmetic  13.5 us (4%)
  starting transfers between devices  10.3 us (3%)
    all_to_all x1, blocking collectives, on_device(): lax.all_to_all(outgoing, 'expert', split_axis=0, concat_axis=0, tiled=True)  101 us
    all_to_all x1, waiting for transfers between devices, on_device(): lax.all_to_all(summed, 'expert', split_axis=0, concat_axis=0, tiled=True)  70.2 us
    all_gather x1, waiting for transfers between devices, on_device(): arrived = lax.all_gather(arrived, 'tensor', axis=2, tiled=True)  21.8 us
    reduce_scatter x1, waiting for transfers between devices, on_device(): lax.psum_scatter(partial_out.astype(jnp.bfloat16), 'tensor', scatter_dime...  21.6 us
    dot_general x1, matrix products, on_device(): jnp.einsum('jecf,efd->jecd', hidden, w_down, preferred_element_type=jnp.f...  13.5 us
    all_to_all x1, starting transfers between devices, on_device(): lax.all_to_all(summed, 'expert', split_axis=0, concat_axis=0, tiled=True)  9.96 us
    dot_general x1, matrix products, on_device(): jnp.einsum('jecd,edf->jecf', grouped, w_up, preferred_element_type=jnp.fl...  9.41 us
    all_gather x1, waiting for transfers between devices, on_device(): piece_rows = lax.all_gather(normed, 'dp', axis=0, tiled=True)  7.91 us
  transfers between devices with their start and end apart: 5, of which 4 were waited for; matrix products, arithmetic and copies ran while one was open for 9% of the time, Pallas kernels for 0%

commit v1 on v0

--- a/solution.py
+++ b/solution.py
@@ -52,7 +52,13 @@
     outgoing = jnp.where(filled[:, None], source_rows[safe_rows], jnp.zeros((), jnp.bfloat16))
     outgoing = outgoing.reshape(EXPERTS, CAP, source_rows.shape[1])
     arrived = lax.all_to_all(outgoing, "expert", split_axis=0, concat_axis=0, tiled=True)
-    arrived = lax.all_gather(arrived, "tensor", axis=2, tiled=True)
+    leaves = []
+    n = lax.psum(1, axis_name="tensor")
+    for p in tuple(range(arrived.ndim)):
+        leaves.append(n if p == 2 else 1)
+    arrived = lax.all_to_all(
+        jnp.tile(arrived, leaves), "tensor", split_axis=2, concat_axis=2, tiled=True
+    )
     slot_count = arrived.shape[1]
     grouped = arrived.reshape(owners, exp_local, slot_count, D)
     gate_value = jnp.einsum("jecd,edf->jecf", grouped, w_gate, preferred_element_type=jnp.float32)

time: 322 us -> 445 us (1.38); the launches traced: 322 us -> 439 us
  local copies, waits for them, and re-layouts: 23.7 us -> 149 us
  waiting for transfers between devices: 122 us -> 96.4 us
  blocking collectives: 101 us -> 119 us
    unnamed x11 -> x13, local copies, waits for them, and re-layouts: 0.96 us -> 77.1 us
    all_to_all x0 -> x2, local copies, waits for them, and re-layouts: none -> 37.4 us  [the longest x1 22.2 us: on_device(): lax.all_to_all(jnp.tile(arrived, leaves), 'tensor', split_axis=2, concat_...]
    all_gather x1 -> x0, waiting for transfers between devices: 21.8 us -> none  [on_device(): arrived = lax.all_gather(arrived, 'tensor', axis=2, tiled=True)]
    all_to_all x0 -> x1, blocking collectives: none -> 17.8 us  [on_device(): lax.all_to_all(jnp.tile(arrived, leaves), 'tensor', split_axis=2, concat_...]
    another operation x0 -> x1, local copies, waits for them, and re-layouts: none -> 11.6 us  [on_device(): jnp.tile(arrived, leaves)]
  transfers between devices with their start and end apart: 5 -> 4, of which waited for: 4 -> 3; matrix products, arithmetic and copies ran while one was open for 9% -> 7% of each run, Pallas kernels for 0% -> 0%
where the time goes in v1:
time: 445 us; the launch traced here: 439 us
  local copies, waits for them, and re-layouts  149 us (33%)
  blocking collectives  119 us (27%)
  waiting for transfers between devices  96.4 us (22%)
  matrix products  36.2 us (8%)
  between operations  15.3 us (3%)
  other arithmetic  13.5 us (3%)
  starting transfers between devices  10.1 us (2%)
    all_to_all x1, blocking collectives, on_device(): lax.all_to_all(outgoing, 'expert', split_axis=0, concat_axis=0, tiled=True)  101 us
    unnamed x13, local copies, waits for them, and re-layouts  77.1 us
    all_to_all x1, waiting for transfers between devices, on_device(): lax.all_to_all(summed, 'expert', split_axis=0, concat_axis=0, tiled=True)  70.2 us
    all_to_all x1, local copies, waits for them, and re-layouts, on_device(): lax.all_to_all(jnp.tile(arrived, leaves), 'tensor', split_axis=2, concat_...  22.2 us
    all_to_all x1, blocking collectives, on_device(): lax.all_to_all(jnp.tile(arrived, leaves), 'tensor', split_axis=2, concat_...  17.8 us
    reduce_scatter x1, waiting for transfers between devices, on_device(): lax.psum_scatter(partial_out.astype(jnp.bfloat16), 'tensor', scatter_dime...  17.6 us
    all_to_all x1, local copies, waits for them, and re-layouts, on_device(): lax.all_to_all(outgoing, 'expert', split_axis=0, concat_axis=0, tiled=True)  15.1 us
    dot_general x1, matrix products, on_device(): jnp.einsum('jecf,efd->jecd', hidden, w_down, preferred_element_type=jnp.f...  13.5 us
  transfers between devices with their start and end apart: 4, of which 3 were waited for; matrix products, arithmetic and copies ran while one was open for 7% of the time, Pallas kernels for 0%

profile of v1, /device:TPU:2, one launch (start us, length us, event | category | flops | bytes accessed | tf_op | source)
XLA Modules:
  0.0 439.5 jit_solution(12934901825076733765)
XLA Ops:
  9.3 1.7 reduce-window.6
  11.7 3.4 scatter_custom_fusion
  15.2 1.3 fusion.22
  16.6 1.3 fusion.24
  17.9 6.0 %gather_fusion = bf16[1536,1280]{1,0:T(8,128)(2,1)} fusion(bf16[128,1280]{1,0:T(8,128)(2,1)S(1)} %constant_dynamic-slice_fusion, s32[2048]{0:T(1024)S(1)} %pad_clamp_fusion), kind=kCustom, calls=%fused_computation | custom fusion | bytes 7870464 | tf_op jit(solution)/shard_map/gather | solution.py:52
  24.0 2.4 broadcast_select_fusion
  26.3 101.1 %all_to_all.15 = bf16[32,48,1280]{2,1,0:T(8,128)(2,1)} all-to-all(bf16[32,48,1280]{2,1,0:T(8,128)(2,1)S(1)} %broadcast_select_fusion), channel_id=1, replica_groups=mesh['dp'=4,'expert'=32,'tensor'=2] {'expert'}, dimensions={0} | all-to-all | bytes 7864320 | tf_op jit(solution)/shard_map/all_to_all | solution.py:54
  127.4 15.1 %copy.22 = bf16[32,48,1280]{1,0,2:T(8,128)(2,1)} copy(bf16[32,48,1280]{2,1,0:T(8,128)(2,1)} %all_to_all.15) | data formatting | bytes 7864320 | tf_op jit(solution)/shard_map/all_to_all | solution.py:54
  142.6 11.6 %tile.4 = bf16[32,48,2,1280]{1,0,3,2:T(8,128)(2,1)} broadcast(bf16[32,48,1280]{1,0,2:T(8,128)(2,1)} %copy.22), dimensions={0,1,3} | broadcast | bytes 11796480 | tf_op jit(solution)/shard_map/tile | solution.py:60
  154.2 43.9 %reshape.138 = bf16[2,2,983040]{2,1,0:T(2,128)(2,1)} reshape(bf16[2560,32,48]{2,1,0:T(8,128)(2,1)} %bitcast.94) | data formatting | bytes 15728640
  198.0 17.8 %all_to_all.16 = bf16[2,2,983040]{2,1,0:T(2,128)(2,1)} all-to-all(bf16[2,2,983040]{2,1,0:T(2,128)(2,1)} %reshape.138), channel_id=1, replica_groups=mesh['dp'=4,'expert'=32,'tensor'=2] {'tensor'}, dimensions={0} | all-to-all | bytes 15728640 | tf_op jit(solution)/shard_map/all_to_all | solution.py:59
  215.8 32.3 %reshape.139 = bf16[2560,32,48]{2,1,0:T(8,128)(2,1)} reshape(bf16[2,2,983040]{2,1,0:T(2,128)(2,1)} %all_to_all.16) | data formatting | bytes 15728640
  248.1 22.2 %copy.23 = bf16[32,48,2560]{2,1,0:T(8,128)(2,1)} copy(bf16[32,48,2560]{1,0,2:T(8,128)(2,1)} %bitcast.93) | data formatting | bytes 15728640 | tf_op jit(solution)/shard_map/all_to_all | solution.py:59
  270.4 9.5 %fusion.13 = f32[32,48,384]{2,1,0:T(8,128)} fusion(bf16[32,48,2560]{2,1,0:T(8,128)(2,1)} %copy.23, bf16[1,2560,384]{2,1,0:T(8,128)(2,1)} %param.15), kind=kOutput, calls=%fused_computation.30 | convolution fusion | flops 3019898880 | bytes 12189696 | tf_op jit(solution)/shard_map/jecd,edf->jecf/dot_general | solution.py:65
  279.9 13.5 %convert_bitcast_fusion = bf16[32,1,48,2560]{3,2,0,1:T(8,128)(2,1)} fusion(bf16[1,384,2560]{2,1,0:T(8,128)(2,1)S(1)} %copy-done, f32[32,48,384]{2,1,0:T(8,128)} %fusion.13, bf16[32,48,2560]{2,1,0:T(8,128)(2,1)} %copy.23, bf16[1,2560,384]{2,1,0:T(8,128)(2,1)} %param.14), kind=kOutput, calls=%fused_computation.3 | convolution fusion | flops 6047268864 | bytes 22020096 | tf_op jit(solution)/shard_map/jecf,efd->jecd/dot_general | solution.py:67
  294.0 17.6 %reduce-scatter.5.cloned.1.call-done = bf16[32,1,48,1280]{3,2,0,1:T(8,128)(2,1)} async-done(((bf16[32,1,48,2560]{3,2,0,1:T(8,128)(2,1)}), bf16[32,1,48,1280]{3,2,0,1:T(8,128)(2,1)}) %reduce-scatter.5.cloned.1.call-update) | async-done | bytes 3932176 | tf_op jit(solution)/shard_map/reduce_scatter | solution.py:68
  311.6 10.0 %all-to-all-start.2 = ((bf16[32,48,1280]{2,1,0:T(8,128)(2,1)}), bf16[32,48,1280]{2,1,0:T(8,128)(2,1)}, u32[]{:S(2)}, u32[]{:S(2)}) async-start(bf16[32,48,1280]{2,1,0:T(8,128)(2,1)} %bitcast.96), calls=%async_computation.4 | async-start | bytes 7864320 | tf_op jit(solution)/shard_map/all_to_all | solution.py:72
  321.6 8.1 %all-gather.2.cloned.1.call-done = bf16[512,2560]{1,0:T(8,128)(2,1)} async-done(((bf16[128,2560]{1,0:T(8,128)(2,1)}), bf16[512,2560]{1,0:T(8,128)(2,1)}) %all-gather.2.cloned.1.call-update) | async-done | bytes 2621456 | tf_op jit(solution)/shard_map/all_gather | solution.py:73
  329.7 3.1 fusion.55
  332.8 2.3 fusion.25
  335.1 1.0 fusion.7
  336.1 1.0 fusion.6
  337.1 1.0 fusion.5
  338.0 1.0 fusion.4
  339.0 1.0 fusion.3
  340.0 1.0 fusion.2
  341.0 1.0 fusion.1
  343.1 70.2 %all-to-all-done.2 = bf16[32,48,1280]{2,1,0:T(8,128)(2,1)} async-done(((bf16[32,48,1280]{2,1,0:T(8,128)(2,1)}), bf16[32,48,1280]{2,1,0:T(8,128)(2,1)}, u32[]{:S(2)}, u32[]{:S(2)}) %all-to-all-start.2) | async-done | bytes 3932192 | tf_op jit(solution)/shard_map/all_to_all | solution.py:72
  413.3 8.1 %gather_fusion.1 = bf16[768,1280]{1,0:T(8,128)(2,1)} fusion(bf16[1536,1280]{1,0:T(8,128)(2,1)} %bitcast.22, s32[1024]{0:T(1024)S(1)} %pad_clamp_fusion.1), kind=kCustom, calls=%fused_computation.1 | custom fusion | bytes 3935232 | tf_op jit(solution)/shard_map/gather | solution.py:93
  421.4 4.5 %reshape.105 = f32[128,6,1280]{2,1,0:T(8,128)} reshape(bf16[768,1280]{1,0:T(8,128)(2,1)} %gather_fusion.1) | data formatting | bytes 5898240 | tf_op jit(solution)/shard_map/convert_element_type | solution.py:93
  425.9 4.1 multiply_reduce_fusion
  430.0 1.8 add_convert_fusion
  (39 shorter events, 4.5 us)
Async XLA Ops:
  7.4 272.5 %copy-start = (bf16[1,384,2560]{2,1,0:T(8,128)(2,1)S(1)}, bf16[1,384,2560]{2,1,0:T(8,128)(2,1)}, u32[]{:S(2)}) copy-start(bf16[1,384,2560]{2,1,0:T(8,128)(2,1)} %param.16) | copy-start | bytes 5898244
  7.4 304.2 %reduce-scatter.5.cloned.1.call-start = ((), (), s32[]{:S(2)}) async-start(), calls=%async_computation.7 | async-start | bytes 11796480 | tf_op jit(solution)/shard_map/reduce_scatter | solution.py:68
  17.9 6.1 %copy-start.1 = (bf16[128,2560]{1,0:T(8,128)(2,1)}, bf16[128,2560]{1,0:T(8,128)(2,1)S(1)}, u32[]{:S(2)}) copy-start(bf16[128,2560]{1,0:T(8,128)(2,1)S(1)} %fusion.24) | copy-start | bytes 1966084
  293.4 36.2 %all-gather.2.cloned.1.call-start = ((), (), s32[]{:S(2)}) async-start(), calls=%async_computation.5 | async-start | bytes 3276800 | tf_op jit(solution)/shard_map/all_gather | solution.py:73
  311.6 101.7 %all-to-all-start.2 = ((bf16[32,48,1280]{2,1,0:T(8,128)(2,1)}), bf16[32,48,1280]{2,1,0:T(8,128)(2,1)}, u32[]{:S(2)}, u32[]{:S(2)}) async-start(bf16[32,48,1280]{2,1,0:T(8,128)(2,1)} %bitcast.96), calls=%async_computation.4 | async-start | bytes 7864320 | tf_op jit(solution)/shard_map/all_to_all | solution.py:72
  321.6 108.5 %reduce-scatter.3.cloned.1.call-start = ((), (), s32[]{:S(2)}) async-start(), calls=%async_computation.6 | async-start | bytes 2949120 | tf_op jit(solution)/shard_map/reduce_scatter | solution.py:86
  329.7 3.1 copy-start.3
  332.8 2.3 copy-start.4
  341.0 2.0 copy-start.2
Sparse Core Ops, SparseCore 0:
  293.6 17.9 reduce-scatter.4
Sparse Core Ops, SparseCore 1:
  295.7 33.9 all-gather.1
  343.1 35.7 reduce-scatter.2
